TPU v7x, 32 devices: a whole 2x2x4 slice. The times are simulated.
32 devices in a mesh: elem: 4 (over y, x), pulse: 8 (over z, core).
Axes of the slice: x: 2, y: 2, z: 4, core: 2. Of those that a mesh axis runs over, the one named last changes fastest.
Arguments:
- echoes: bfloat16 [2, 2048, 256, 256], P(None, 'elem', 'pulse'), may hold values from -6 to 6
- keep_mask: int32 [256, 8], P('pulse'), may hold values from 0 to 1, as said below
- steer_index: int32 [512], replicated, may hold values from 0 to 1023
- element_position: float32 [2048], replicated, may hold values from 0 to 1024
- element_gain: float32 [2, 2048], replicated, may hold values from -4 to 4
- steer_sines: float32 [1024], replicated, may hold values from -1 to 1
Outputs:
- doppler_power: float32 [512, 256, 256], P('pulse', None, 'elem')
Inputs may be any that keep to these rules, and one draw needn't show every extreme that they name: `keep_mask`: in each masking block, each aligned run of 32 pulses keeps at most 24 pulses, and at least one; in every masking block some run keeps exactly 24.
All inputs are finite; a program needn't handle non-finite values.
Results may differ from a plain program's by a relative error of at most 0.005.
Values may be sent and summed in bfloat16 or wider, within the bound.
No kernel may reach another device: no remote copies, remote signals or barrier semaphores. Data moves between devices by JAX's collectives and lax.ppermute only.
A program may use at most 128 MiB of HBM per device.

v0:
```python
import math
import jax
import jax.numpy as jnp
from jax import lax
from jax.sharding import PartitionSpec as P

E = 2048
P_SIZE = 256
RBLK = 32


def steering(element_position, element_gain, sines):
    phase = 2.0 * math.pi * element_position[:, None] * sines[None, :]
    cosine = jnp.cos(phase)
    sine = jnp.sin(phase)
    factor = 1.0 / math.sqrt(E)
    real = (element_gain[0][:, None] * cosine + element_gain[1][:, None] * sine) * factor
    imag = (element_gain[1][:, None] * cosine - element_gain[0][:, None] * sine) * factor
    return (real.astype(jnp.bfloat16), imag.astype(jnp.bfloat16))


def tables(count):
    index = jnp.arange(count, dtype=jnp.int32)
    angle = 2.0 * math.pi * (index[:, None] * index[None, :] % count).astype(jnp.float32) / count
    taper = 0.54 - 0.46 * jnp.cos(2.0 * math.pi * index.astype(jnp.float32) / (count - 1))
    taper = taper / math.sqrt(count)
    cos_table = jnp.cos(angle) * taper[None, :]
    sin_table = jnp.sin(angle) * taper[None, :]
    upper = jnp.concatenate((cos_table, sin_table), axis=1)
    lower = jnp.concatenate((-sin_table, cos_table), axis=1)
    transform = jnp.concatenate((upper, lower), axis=0)
    high = transform.astype(jnp.bfloat16)
    low = (transform - high.astype(jnp.float32)).astype(jnp.bfloat16)
    return (high, low)


def contract(left, right):
    return lax.dot_general(
        left, right, (((0,), (0,)), ((), ())), preferred_element_type=jnp.float32
    )


def per_device(echoes, keep_mask, steer_index, element_position, element_gain, steer_sines):
    choices_all = jnp.arange(steer_sines.shape[0], dtype=jnp.int32)
    sines = jnp.sum(
        jnp.where(steer_index[:, None] == choices_all[None, :], steer_sines[None, :], 0.0), axis=1
    )
    weight_re, weight_im = steering(element_position, element_gain, sines)
    high, low = tables(P_SIZE)
    count = P_SIZE
    groups = lax.axis_size("elem")
    local_elems = echoes.shape[1]
    local_pulses = echoes.shape[2]
    total_cells = echoes.shape[3]
    cells = total_cells // groups
    blocks_all = keep_mask.shape[1]
    kept_slots = (3 * local_pulses + 3) // 4
    offset = lax.axis_index("elem") * cells
    rank = jnp.cumsum(keep_mask, axis=0) - 1
    slot_ids = jnp.arange(kept_slots, dtype=jnp.int32)
    selector = (
        (keep_mask[None, :, :] == 1) & (rank[None, :, :] == slot_ids[:, None, None])
    ).astype(jnp.bfloat16)
    shaped5 = echoes.reshape(2, local_elems, local_pulses, blocks_all, total_cells // blocks_all)
    prepared = jnp.einsum("spk,cepkr->ceskr", selector, shaped5, preferred_element_type=jnp.float32)
    prepared = prepared.astype(jnp.bfloat16).reshape(2, local_elems, kept_slots, total_cells)
    turned = lax.all_to_all(prepared, "elem", split_axis=3, concat_axis=1, tiled=True)
    span = turned.shape[3]
    flat = turned.reshape(2, turned.shape[1], turned.shape[2] * span)
    real = contract(weight_re, flat[0]) - contract(weight_im, flat[1])
    imag = contract(weight_re, flat[1]) + contract(weight_im, flat[0])
    real = real.astype(jnp.bfloat16).reshape(-1, turned.shape[2], span)
    imag = imag.astype(jnp.bfloat16).reshape(-1, turned.shape[2], span)
    packed_re = real
    packed_im = imag
    block_ids = jnp.arange(blocks_all, dtype=jnp.int32)
    onehot = (
        (offset + jnp.arange(cells, dtype=jnp.int32))[:, None] // RBLK == block_ids[None, :]
    ).astype(jnp.bfloat16)
    spread = jnp.einsum("spk,nk->spn", selector, onehot, preferred_element_type=jnp.float32).astype(
        jnp.bfloat16
    )
    real = jnp.einsum("spn,bsn->bpn", spread, packed_re, preferred_element_type=jnp.float32).astype(
        jnp.bfloat16
    )
    imag = jnp.einsum("spn,bsn->bpn", spread, packed_im, preferred_element_type=jnp.float32).astype(
        jnp.bfloat16
    )
    beam_re = lax.all_to_all(real, "pulse", split_axis=0, concat_axis=1, tiled=True)
    beam_im = lax.all_to_all(imag, "pulse", split_axis=0, concat_axis=1, tiled=True)
    total = None
    for table in (high, low):
        part_re = jnp.einsum(
            "fp,bpn->bfn", table[:, :count], beam_re, preferred_element_type=jnp.float32
        )
        part_im = jnp.einsum(
            "fp,bpn->bfn", table[:, count:], beam_im, preferred_element_type=jnp.float32
        )
        total = part_re + part_im if total is None else total + part_re + part_im
    doppler_real = total[:, :count]
    doppler_imag = total[:, count:]
    return doppler_real * doppler_real + doppler_imag * doppler_imag


def solution(mesh):
    placed = (P(None, "elem", "pulse", None), P("pulse", None), P(), P(), P(), P())
    return jax.shard_map(
        per_device, mesh=mesh, in_specs=placed, out_specs=P("pulse", None, "elem"), check_vma=False
    )
```

profile of v0, /device:TPU:0, one launch (start us, length us, event | category | flops | bytes accessed | tf_op | source)
XLA Modules:
  0.0 494.8 jit_solution(7825158454604493364)
XLA Ops:
  1.6 26.3 %copy.87 = bf16[2,512,32,256]{1,3,2,0:T(8,128)(2,1)} copy(bf16[2,512,32,256]{3,2,1,0:T(8,128)(2,1)} %param.6) | data formatting | bytes 33554432 | tf_op args[0]
  27.9 21.7 %convert_bitcast_fusion = bf16[2,512,24,8,32]{1,2,4,0,3:T(8,128)(2,1)} fusion(bf16[2,512,32,8,32]{1,4,3,2,0:T(8,128)(2,1)} %bitcast.62, pred[24,32,8,1,1]{1,2,0,4,3:T(8,128)(4,1)S(1)} %fusion.38), kind=kOutput, calls=%fused_computation.2 | convolution fusion | flops 408944640 | bytes 29366272 | tf_op jit(solution)/shard_map/spk,cepkr->ceskr/dot_general | solution.py:65
  49.6 9.4 %copy.90 = bf16[2,512,24,8,32]{1,4,3,2,0:T(8,128)(2,1)S(1)} copy(bf16[2,512,24,8,32]{1,2,4,0,3:T(8,128)(2,1)} %convert_bitcast_fusion) | data formatting | bytes 25165824 | tf_op jit(solution)/shard_map/convert_element_type | solution.py:66
  59.0 23.9 %copy.91 = bf16[2,512,24,256]{1,2,0,3:T(8,128)(2,1)} copy(bf16[2,512,24,256]{1,3,2,0:T(8,128)(2,1)S(1)} %bitcast.64) | data formatting | bytes 25165824 | tf_op jit(solution)/shard_map/reshape | solution.py:66
  83.0 6.4 %all-to-all-start = ((bf16[2,512,24,256]{1,2,0,3:T(8,128)(2,1)}), bf16[2,512,24,256]{1,2,0,3:T(8,128)(2,1)}, u32[]{:S(2)}, u32[]{:S(2)}) async-start(bf16[2,512,24,256]{1,2,0,3:T(8,128)(2,1)} %copy.91), calls=%async_computation | async-start | bytes 25165824 | tf_op jit(solution)/shard_map/all_to_all | solution.py:67
  90.4 137.9 %all-to-all-done = bf16[2,512,24,256]{1,2,0,3:T(8,128)(2,1)} async-done(((bf16[2,512,24,256]{1,2,0,3:T(8,128)(2,1)}), bf16[2,512,24,256]{1,2,0,3:T(8,128)(2,1)}, u32[]{:S(2)}, u32[]{:S(2)}) %all-to-all-start) | async-done | bytes 12582944 | tf_op jit(solution)/shard_map/all_to_all | solution.py:67
  228.3 9.3 %copy.92 = bf16[2,512,24,256]{1,3,2,0:T(8,128)(2,1)S(1)} copy(bf16[2,512,24,256]{1,2,0,3:T(8,128)(2,1)} %all-to-all-done) | data formatting | bytes 25165824 | tf_op jit(solution)/shard_map/all_to_all | solution.py:67
  242.9 8.5 %copy.94 = bf16[1,4,512,24,64]{2,1,4,3,0:T(4,128)(2,1)S(1)} copy(bf16[1,4,512,24,64]{2,4,1,3,0:T(8,128)(2,1)} %get-tuple-element.5) | data formatting | bytes 12582912 | tf_op jit(solution)/shard_map/slice | solution.py:70
  256.8 8.7 %copy.93 = bf16[1,4,512,24,64]{2,1,4,3,0:T(4,128)(2,1)S(1)} copy(bf16[1,4,512,24,64]{2,4,1,3,0:T(8,128)(2,1)} %get-tuple-element.6) | data formatting | bytes 12582912 | tf_op jit(solution)/shard_map/slice | solution.py:70
  268.2 18.6 %fusion.21 = f32[512,1536]{1,0:T(8,128)S(1)} fusion(bf16[2048,1536]{0,1:T(8,128)(2,1)S(1)} %bitcast.73, f32[2048]{0:T(1024)S(1)} %bitcast.85, f32[512]{0:T(512)S(1)} %select_reduce_fusion, f32[2048]{0:T(1024)S(1)} %broadcast_multiply_fusion, f32[2048]{0:T(1024)S(1)} %bitcast.81), kind=kOutput, calls=%fused_computation.28 | convolution fusion | flops 3227516928 | bytes 9463808 | tf_op jit(solution)/shard_map/dot_general | solution.py:38
  286.9 18.3 %fusion.15 = bf16[512,1536]{1,0:T(8,128)(2,1)S(1)} fusion(f32[512,1536]{1,0:T(8,128)S(1)} %fusion.21, bf16[2048,1536]{0,1:T(8,128)(2,1)S(1)} %bitcast.78, f32[2048]{0:T(1024)S(1)} %bitcast.86, f32[512]{0:T(512)S(1)} %select_reduce_fusion, f32[2048]{0:T(1024)S(1)} %broadcast_multiply_fusion, f32[2048]{0:T(1024)S(1)} %bitcast.82), kind=kOutput, calls=%fused_computation.21 | convolution fusion | flops 3229089792 | bytes 11036672 | tf_op jit(solution)/shard_map/dot_general | solution.py:38
  309.6 7.8 %copy.98 = bf16[512,32,64]{2,1,0:T(8,128)(2,1)} copy(bf16[512,32,64]{0,1,2:T(8,128)(2,1)S(1)} %convert_bitcast_fusion.2) | data formatting | bytes 4194304 | tf_op jit(solution)/shard_map/convert_element_type | solution.py:83
  317.4 7.6 %reshape.90 = bf16[8,2,65536]{2,1,0:T(2,128)(2,1)} reshape(bf16[512,32,64]{2,1,0:T(8,128)(2,1)} %copy.98) | data formatting | bytes 4194304
  330.2 21.1 %fusion.19 = f32[512,1536]{1,0:T(8,128)S(1)} fusion(bf16[2048,1536]{0,1:T(8,128)(2,1)} %bitcast.75, f32[2048]{0:T(1024)S(1)} %bitcast.87, f32[512]{0:T(512)S(1)} %select_reduce_fusion, f32[2048]{0:T(1024)S(1)} %broadcast_multiply_fusion, f32[2048]{0:T(1024)S(1)} %bitcast.83), kind=kOutput, calls=%fused_computation.27 | convolution fusion | flops 3227516928 | bytes 9463808 | tf_op jit(solution)/shard_map/dot_general | solution.py:38
  351.4 22.4 %fusion.16 = bf16[512,1536]{1,0:T(8,128)(2,1)} fusion(f32[512,1536]{1,0:T(8,128)S(1)} %fusion.19, bf16[2048,1536]{0,1:T(8,128)(2,1)} %bitcast.74, f32[2048]{0:T(1024)S(1)} %bitcast.88, f32[512]{0:T(512)S(1)} %select_reduce_fusion, f32[2048]{0:T(1024)S(1)} %broadcast_multiply_fusion, f32[2048]{0:T(1024)S(1)} %bitcast.84), kind=kOutput, calls=%fused_computation.22 | convolution fusion | flops 3229089792 | bytes 11036672 | tf_op jit(solution)/shard_map/dot_general | solution.py:38
  380.5 8.8 %copy.104 = bf16[512,32,64]{2,1,0:T(8,128)(2,1)} copy(bf16[512,32,64]{0,1,2:T(8,128)(2,1)} %convert_bitcast_fusion.1) | data formatting | bytes 4194304 | tf_op jit(solution)/shard_map/convert_element_type | solution.py:86
  389.2 7.6 %reshape.92 = bf16[8,2,65536]{2,1,0:T(2,128)(2,1)} reshape(bf16[512,32,64]{2,1,0:T(8,128)(2,1)} %copy.104) | data formatting | bytes 4194304
  408.1 5.4 %copy.99 = bf16[8,64,32,64]{3,2,0,1:T(8,128)(2,1)} copy(bf16[8,64,32,64]{3,2,1,0:T(8,128)(2,1)} %bitcast.71) | data formatting | bytes 4194304 | tf_op jit(solution)/shard_map/all_to_all | solution.py:89
  413.5 37.5 %all-to-all-done.2 = bf16[8,2,65536]{2,1,0:T(2,128)(2,1)} async-done(((bf16[8,2,65536]{2,1,0:T(2,128)(2,1)}), bf16[8,2,65536]{2,1,0:T(2,128)(2,1)}, u32[]{:S(2)}, u32[]{:S(2)}) %all-to-all-start.2) | async-done | bytes 2097184 | tf_op jit(solution)/shard_map/all_to_all | solution.py:90
  451.0 7.6 %reshape.93 = bf16[512,32,64]{2,1,0:T(8,128)(2,1)} reshape(bf16[8,2,65536]{2,1,0:T(2,128)(2,1)} %all-to-all-done.2) | data formatting | bytes 4194304
  464.4 5.6 %fusion.31 = f32[64,64,512]{2,1,0:T(8,128)} fusion(bf16[64,256,64]{2,1,0:T(8,128)(2,1)S(1)} %bitcast.65, bf16[512,512]{1,0:T(8,128)(2,1)S(1)} %fusion.25), kind=kOutput, calls=%fused_computation.47 | convolution fusion | flops 1073741824 | bytes 12845056 | tf_op jit(solution)/shard_map/fp,bpn->bfn/dot_general | solution.py:93
  470.0 5.6 %fusion.29 = f32[64,64,512]{2,1,0:T(8,128)} fusion(bf16[64,256,64]{2,1,0:T(8,128)(2,1)S(1)} %bitcast.66, bf16[512,512]{1,0:T(8,128)(2,1)S(1)} %subtract_convert_fusion), kind=kOutput, calls=%fused_computation.43 | convolution fusion | flops 1073741824 | bytes 12845056 | tf_op jit(solution)/shard_map/fp,bpn->bfn/dot_general | solution.py:93
  475.7 12.0 %add_bitcast_fusion = f32[64,512,64]{1,2,0:T(8,128)} fusion(f32[64,64,512]{2,1,0:T(8,128)} %fusion.29, f32[64,64,512]{2,1,0:T(8,128)} %fusion.31, f32[64,64,512]{2,1,0:T(8,128)S(1)} %fusion.30, bf16[64,256,64]{2,1,0:T(8,128)(2,1)S(1)} %bitcast.68, bf16[512,512]{1,0:T(8,128)(2,1)S(1)} %subtract_convert_fusion), kind=kOutput, calls=%fused_computation.3 | convolution fusion | flops 1080033280 | bytes 38010880 | tf_op jit(solution)/shard_map/fp,bpn->bfn/dot_general | solution.py:96
  487.7 6.7 %fusion.14 = f32[64,256,64]{1,2,0:T(8,128)} fusion(f32[64,512,64]{1,2,0:T(8,128)} %add_bitcast_fusion), kind=kLoop, calls=%fused_computation.17 | loop fusion | flops 3145728 | bytes 12582912 | tf_op jit(solution)/shard_map/add | solution.py:102
  (46 shorter events, 49.3 us)
Async XLA Ops:
  83.0 7.1 %copy-start.4 = (f32[1024]{0:T(1024)S(1)}, f32[1024]{0:T(1024)}, u32[]{:S(2)}) copy-start(f32[1024]{0:T(1024)} %param.11) | copy-start | bytes 12292
  83.0 7.1 %copy-start.5 = (s32[512]{0:T(512)S(1)}, s32[512]{0:T(512)}, u32[]{:S(2)}) copy-start(s32[512]{0:T(512)} %param.8) | copy-start | bytes 6148
  83.0 7.4 %copy-start.3 = (f32[2048]{0:T(1024)S(1)}, f32[2048]{0:T(1024)}, u32[]{:S(2)}) copy-start(f32[2048]{0:T(1024)} %param.9) | copy-start | bytes 24580
  83.0 7.4 %copy-start.2 = (f32[2,2048]{1,0:T(2,128)S(1)}, f32[2,2048]{1,0:T(2,128)}, u32[]{:S(2)}) copy-start(f32[2,2048]{1,0:T(2,128)} %param.10) | copy-start | bytes 49156
  83.0 145.3 %all-to-all-start = ((bf16[2,512,24,256]{1,2,0,3:T(8,128)(2,1)}), bf16[2,512,24,256]{1,2,0,3:T(8,128)(2,1)}, u32[]{:S(2)}, u32[]{:S(2)}) async-start(bf16[2,512,24,256]{1,2,0,3:T(8,128)(2,1)} %copy.91), calls=%async_computation | async-start | bytes 25165824 | tf_op jit(solution)/shard_map/all_to_all | solution.py:67
  265.4 21.4 %slice-start = ((s8[6291456]{0:T(1024)(128)(4,1)}), s8[4194304]{0:T(1024)(128)(4,1)S(1)}, s32[]{:S(2)}) async-start(s8[6291456]{0:T(1024)(128)(4,1)} %bitcast.76), calls=%async_computation.3 | async-start | bytes 8388608
  268.2 18.7 %copy-start.1 = (bf16[192,8,4,512]{3,1,2,0:T(8,128)(2,1)}, bf16[192,8,4,512]{3,1,2,0:T(8,128)(2,1)S(1)}, u32[]{:S(2)}) copy-start(bf16[192,8,4,512]{3,1,2,0:T(8,128)(2,1)S(1)} %copy.116) | copy-start | bytes 18874372
  268.2 18.7 %slice-start.1 = ((s8[6291456]{0:T(1024)(128)(4,1)}), s8[2097152]{0:T(1024)(128)(4,1)S(1)}, s32[]{:S(2)}) async-start(s8[6291456]{0:T(1024)(128)(4,1)} %bitcast.76), calls=%async_computation.4 | async-start | bytes 4194304
  325.0 71.8 %all-to-all-start.1 = ((bf16[8,2,65536]{2,1,0:T(2,128)(2,1)}), bf16[8,2,65536]{2,1,0:T(2,128)(2,1)S(1)}, u32[]{:S(2)}, u32[]{:S(2)}) async-start(bf16[8,2,65536]{2,1,0:T(2,128)(2,1)} %reshape.90), calls=%async_computation.1 | async-start | bytes 4194304 | tf_op jit(solution)/shard_map/all_to_all | solution.py:89
  396.8 54.2 %all-to-all-start.2 = ((bf16[8,2,65536]{2,1,0:T(2,128)(2,1)}), bf16[8,2,65536]{2,1,0:T(2,128)(2,1)}, u32[]{:S(2)}, u32[]{:S(2)}) async-start(bf16[8,2,65536]{2,1,0:T(2,128)(2,1)} %reshape.92), calls=%async_computation.2 | async-start | bytes 4194304 | tf_op jit(solution)/shard_map/all_to_all | solution.py:90
  462.0 2.4 copy-start
where the time goes:
time: 503 us; the launch traced here: 495 us
  waiting for transfers between devices  175 us (35%)
  local copies, waits for them, and re-layouts  158 us (31%)
  matrix products  135 us (27%)
  starting transfers between devices  16.8 us (3%)
  other arithmetic  9.09 us (2%)
    all_to_all x1, waiting for transfers between devices, per_device(): lax.all_to_all(prepared, 'elem', split_axis=3, concat_axis=1, tiled=True)  138 us
    dot_general x4, matrix products, contract(): lax.dot_general(left, right, (((0,), (0,)), ((), ())), preferred_element_...  80.4 us
    unnamed x24, local copies, waits for them, and re-layouts  62.8 us
    all_to_all x1, waiting for transfers between devices, per_device(): lax.all_to_all(imag, 'pulse', split_axis=0, concat_axis=1, tiled=True)  37.5 us
    reshape x1, local copies, waits for them, and re-layouts, per_device(): prepared.astype(jnp.bfloat16)  23.9 us
    slice x3, local copies, waits for them, and re-layouts, per_device(): real = contract(weight_re, flat[0]) - contract(weight_im, flat[1])  22.5 us
    dot_general x1, matrix products, per_device(): jnp.einsum('spk,cepkr->ceskr', selector, shaped5, preferred_element_type=...  21.7 us
    dot_general x2, matrix products, per_device(): jnp.einsum('fp,bpn->bfn', table[:, count:], beam_im, preferred_element_ty...  14.4 us
  transfers between devices with their start and end apart: 3, of which 2 were waited for; matrix products, arithmetic and copies ran while one was open for 16% of the time, Pallas kernels for 0%

commit v1 on v0

--- a/solution.py
+++ b/solution.py
@@ -64,7 +64,10 @@
     shaped5 = echoes.reshape(2, local_elems, local_pulses, blocks_all, total_cells // blocks_all)
     prepared = jnp.einsum("spk,cepkr->ceskr", selector, shaped5, preferred_element_type=jnp.float32)
     prepared = prepared.astype(jnp.bfloat16).reshape(2, local_elems, kept_slots, total_cells)
-    turned = lax.all_to_all(prepared, "elem", split_axis=3, concat_axis=1, tiled=True)
+    turned = jnp.concatenate(
+        lax.all_to_all(jnp.stack(jnp.split(prepared, lax.axis_size("elem"), axis=3)), "elem", 0, 0),
+        axis=1,
+    )
     span = turned.shape[3]
     flat = turned.reshape(2, turned.shape[1], turned.shape[2] * span)
     real = contract(weight_re, flat[0]) - contract(weight_im, flat[1])

time: 503 us -> 484 us (0.962)
  local copies, waits for them, and re-layouts: 158 us -> 132 us
  other arithmetic: 9.09 us -> 14.7 us
    reshape x1 -> x0, local copies, waits for them, and re-layouts: 23.9 us -> none  [per_device(): prepared.astype(jnp.bfloat16)]
    all_to_all x1 -> x0, local copies, waits for them, and re-layouts: 9.3 us -> none  [per_device(): lax.all_to_all(prepared, 'elem', split_axis=3, concat_axis=1, tiled=True)]
    another operation x0 -> x1, other arithmetic: none -> 5.6 us  [per_device(): jnp.stack(jnp.split(prepared, lax.axis_size('elem'), axis=3))]
    slice x3, local copies, waits for them, and re-layouts: 22.5 us -> 27.9 us  [per_device(): real = contract(weight_re, flat[0]) - contract(weight_im, flat[1])]
  transfers between devices with their start and end apart: 3 -> 3, of which waited for: 2 -> 2; matrix products, arithmetic and copies ran while one was open for 16% -> 17% of each run, Pallas kernels for 0% -> 0%
where the time goes in v1:
time: 484 us; the launch traced here: 474 us
  waiting for transfers between devices  175 us (36%)
  matrix products  135 us (28%)
  local copies, waits for them, and re-layouts  132 us (27%)
  starting transfers between devices  17 us (4%)
  other arithmetic  14.7 us (3%)
    all_to_all x1, waiting for transfers between devices, per_device(): lax.all_to_all(jnp.stack(jnp.split(prepared, lax.axis_size('elem'), axis=...  138 us
    dot_general x4, matrix products, contract(): lax.dot_general(left, right, (((0,), (0,)), ((), ())), preferred_element_...  80.5 us
    unnamed x24, local copies, waits for them, and re-layouts  62.8 us
    all_to_all x1, waiting for transfers between devices, per_device(): lax.all_to_all(imag, 'pulse', split_axis=0, concat_axis=1, tiled=True)  37.5 us
    slice x3, local copies, waits for them, and re-layouts, per_device(): real = contract(weight_re, flat[0]) - contract(weight_im, flat[1])  27.9 us
    dot_general x1, matrix products, per_device(): jnp.einsum('spk,cepkr->ceskr', selector, shaped5, preferred_element_type=...  21.7 us
    dot_general x2, matrix products, per_device(): jnp.einsum('fp,bpn->bfn', table[:, count:], beam_im, preferred_element_ty...  14.4 us
    dot_general x2, matrix products, per_device(): jnp.einsum('fp,bpn->bfn', table[:, :count], beam_re, preferred_element_ty...  11.3 us
  transfers between devices with their start and end apart: 3, of which 2 were waited for; matrix products, arithmetic and copies ran while one was open for 17% of the time, Pallas kernels for 0%

profile of v1, /device:TPU:0, one launch (start us, length us, event | category | flops | bytes accessed | tf_op | source)
XLA Modules:
  0.0 474.2 jit_solution(3742169964461354859)
XLA Ops:
  1.6 26.3 %copy.83 = bf16[2,512,32,256]{1,3,2,0:T(8,128)(2,1)} copy(bf16[2,512,32,256]{3,2,1,0:T(8,128)(2,1)} %param.6) | data formatting | bytes 33554432 | tf_op args[0]
  27.9 21.7 %convert_bitcast_fusion = bf16[2,512,24,8,32]{1,2,4,0,3:T(8,128)(2,1)} fusion(bf16[2,512,32,8,32]{1,4,3,2,0:T(8,128)(2,1)} %bitcast.68, pred[24,32,8,1,1]{1,2,0,4,3:T(8,128)(4,1)S(1)} %fusion.38), kind=kOutput, calls=%fused_computation.3 | convolution fusion | flops 408944640 | bytes 29366272 | tf_op jit(solution)/shard_map/spk,cepkr->ceskr/dot_general | solution.py:65
  49.6 9.4 %copy.86 = bf16[2,512,24,8,32]{1,4,3,2,0:T(8,128)(2,1)S(1)} copy(bf16[2,512,24,8,32]{1,2,4,0,3:T(8,128)(2,1)} %convert_bitcast_fusion) | data formatting | bytes 25165824 | tf_op jit(solution)/shard_map/convert_element_type | solution.py:66
  60.7 5.6 %pad_maximum_fusion = bf16[4,2,512,24,64]{2,4,3,1,0:T(8,128)(2,1)} fusion(bf16[1,2,512,24,64]{2,4,3,1,0:T(8,128)(2,1)S(1)} %get-tuple-element.8, bf16[1,2,512,24,64]{2,4,3,1,0:T(8,128)(2,1)S(1)} %get-tuple-element.9, bf16[1,2,512,24,64]{2,4,3,1,0:T(8,128)(2,1)S(1)} %get-tuple-element.10, bf16[1,2,512,24,64]{2,4,3,1,0:T(8,128)(2,1)S(1)} %get-tuple-element.7), kind=kLoop, calls=%fused_computation.2 | loop fusion | flops 18874368 | bytes 25165824 | tf_op jit(solution)/shard_map/stack | solution.py:68
  66.3 6.4 %all-to-all-start = ((bf16[4,2,512,24,64]{2,4,3,1,0:T(8,128)(2,1)}), bf16[4,2,512,24,64]{2,4,3,1,0:T(8,128)(2,1)}, u32[]{:S(2)}, u32[]{:S(2)}) async-start(bf16[4,2,512,24,64]{2,4,3,1,0:T(8,128)(2,1)} %pad_maximum_fusion), calls=%async_computation | async-start | bytes 25165824 | tf_op jit(solution)/shard_map/all_to_all | solution.py:68
  73.8 137.9 %all-to-all-done = bf16[4,2,512,24,64]{2,4,3,1,0:T(8,128)(2,1)} async-done(((bf16[4,2,512,24,64]{2,4,3,1,0:T(8,128)(2,1)}), bf16[4,2,512,24,64]{2,4,3,1,0:T(8,128)(2,1)}, u32[]{:S(2)}, u32[]{:S(2)}) %all-to-all-start) | async-done | bytes 12582944 | tf_op jit(solution)/shard_map/all_to_all | solution.py:68
  211.6 10.7 %fusion.49 = (bf16[1,4,512,24,64]{2,4,3,0,1:T(8,128)(2,1)}, bf16[1,4,512,24,64]{2,4,3,0,1:T(8,128)(2,1)}) fusion(bf16[2,4,512,24,64]{2,4,3,0,1:T(8,128)(2,1)} %bitcast.10), kind=kLoop, calls=%fused_computation.80 | loop fusion | bytes 25165824 | tf_op jit(solution)/shard_map/slice | solution.py:73
  222.3 8.5 %copy.88 = bf16[1,4,512,24,64]{2,1,4,3,0:T(4,128)(2,1)S(1)} copy(bf16[1,4,512,24,64]{2,4,3,0,1:T(8,128)(2,1)} %get-tuple-element.5) | data formatting | bytes 12582912 | tf_op jit(solution)/shard_map/slice | solution.py:73
  236.2 8.7 %copy.87 = bf16[1,4,512,24,64]{2,1,4,3,0:T(4,128)(2,1)S(1)} copy(bf16[1,4,512,24,64]{2,4,3,0,1:T(8,128)(2,1)} %get-tuple-element.6) | data formatting | bytes 12582912 | tf_op jit(solution)/shard_map/slice | solution.py:73
  247.7 18.6 %fusion.21 = f32[512,1536]{1,0:T(8,128)S(1)} fusion(bf16[2048,1536]{0,1:T(8,128)(2,1)S(1)} %bitcast.78, f32[2048]{0:T(1024)S(1)} %bitcast.90, f32[512]{0:T(512)S(1)} %select_reduce_fusion, f32[2048]{0:T(1024)S(1)} %broadcast_multiply_fusion, f32[2048]{0:T(1024)S(1)} %bitcast.86), kind=kOutput, calls=%fused_computation.33 | convolution fusion | flops 3227516928 | bytes 9463808 | tf_op jit(solution)/shard_map/dot_general | solution.py:38
  266.3 18.3 %fusion.15 = bf16[512,1536]{1,0:T(8,128)(2,1)S(1)} fusion(f32[512,1536]{1,0:T(8,128)S(1)} %fusion.21, bf16[2048,1536]{0,1:T(8,128)(2,1)S(1)} %bitcast.83, f32[2048]{0:T(1024)S(1)} %bitcast.91, f32[512]{0:T(512)S(1)} %select_reduce_fusion, f32[2048]{0:T(1024)S(1)} %broadcast_multiply_fusion, f32[2048]{0:T(1024)S(1)} %bitcast.87), kind=kOutput, calls=%fused_computation.26 | convolution fusion | flops 3229089792 | bytes 11036672 | tf_op jit(solution)/shard_map/dot_general | solution.py:38
  289.0 7.8 %copy.92 = bf16[512,32,64]{2,1,0:T(8,128)(2,1)} copy(bf16[512,32,64]{0,1,2:T(8,128)(2,1)S(1)} %convert_bitcast_fusion.2) | data formatting | bytes 4194304 | tf_op jit(solution)/shard_map/convert_element_type | solution.py:86
  296.8 7.6 %reshape.92 = bf16[8,2,65536]{2,1,0:T(2,128)(2,1)} reshape(bf16[512,32,64]{2,1,0:T(8,128)(2,1)} %copy.92) | data formatting | bytes 4194304
  309.8 20.9 %fusion.19 = f32[512,1536]{1,0:T(8,128)S(1)} fusion(bf16[2048,1536]{0,1:T(8,128)(2,1)} %bitcast.80, f32[2048]{0:T(1024)S(1)} %bitcast.92, f32[512]{0:T(512)S(1)} %select_reduce_fusion, f32[2048]{0:T(1024)S(1)} %broadcast_multiply_fusion, f32[2048]{0:T(1024)S(1)} %bitcast.88), kind=kOutput, calls=%fused_computation.32 | convolution fusion | flops 3227516928 | bytes 9463808 | tf_op jit(solution)/shard_map/dot_general | solution.py:38
  330.8 22.6 %fusion.16 = bf16[512,1536]{1,0:T(8,128)(2,1)} fusion(f32[512,1536]{1,0:T(8,128)S(1)} %fusion.19, bf16[2048,1536]{0,1:T(8,128)(2,1)} %bitcast.79, f32[2048]{0:T(1024)S(1)} %bitcast.93, f32[512]{0:T(512)S(1)} %select_reduce_fusion, f32[2048]{0:T(1024)S(1)} %broadcast_multiply_fusion, f32[2048]{0:T(1024)S(1)} %bitcast.89), kind=kOutput, calls=%fused_computation.27 | convolution fusion | flops 3229089792 | bytes 11036672 | tf_op jit(solution)/shard_map/dot_general | solution.py:38
  360.1 8.8 %copy.98 = bf16[512,32,64]{2,1,0:T(8,128)(2,1)} copy(bf16[512,32,64]{0,1,2:T(8,128)(2,1)} %convert_bitcast_fusion.1) | data formatting | bytes 4194304 | tf_op jit(solution)/shard_map/convert_element_type | solution.py:89
  368.9 7.6 %reshape.94 = bf16[8,2,65536]{2,1,0:T(2,128)(2,1)} reshape(bf16[512,32,64]{2,1,0:T(8,128)(2,1)} %copy.98) | data formatting | bytes 4194304
  387.8 5.4 %copy.93 = bf16[8,64,32,64]{3,2,0,1:T(8,128)(2,1)} copy(bf16[8,64,32,64]{3,2,1,0:T(8,128)(2,1)} %bitcast.76) | data formatting | bytes 4194304 | tf_op jit(solution)/shard_map/all_to_all | solution.py:92
  393.2 37.5 %all-to-all-done.2 = bf16[8,2,65536]{2,1,0:T(2,128)(2,1)} async-done(((bf16[8,2,65536]{2,1,0:T(2,128)(2,1)}), bf16[8,2,65536]{2,1,0:T(2,128)(2,1)}, u32[]{:S(2)}, u32[]{:S(2)}) %all-to-all-start.2) | async-done | bytes 2097184 | tf_op jit(solution)/shard_map/all_to_all | solution.py:93
  430.7 7.5 %reshape.95 = bf16[512,32,64]{2,1,0:T(8,128)(2,1)} reshape(bf16[8,2,65536]{2,1,0:T(2,128)(2,1)} %all-to-all-done.2) | data formatting | bytes 4194304
  444.0 5.6 %fusion.31 = f32[64,64,512]{2,1,0:T(8,128)} fusion(bf16[64,256,64]{2,1,0:T(8,128)(2,1)S(1)} %bitcast.70, bf16[512,512]{1,0:T(8,128)(2,1)S(1)} %fusion.25), kind=kOutput, calls=%fused_computation.52 | convolution fusion | flops 1073741824 | bytes 12845056 | tf_op jit(solution)/shard_map/fp,bpn->bfn/dot_general | solution.py:96
  449.6 5.6 %fusion.29 = f32[64,64,512]{2,1,0:T(8,128)} fusion(bf16[64,256,64]{2,1,0:T(8,128)(2,1)S(1)} %bitcast.71, bf16[512,512]{1,0:T(8,128)(2,1)S(1)} %subtract_convert_fusion), kind=kOutput, calls=%fused_computation.48 | convolution fusion | flops 1073741824 | bytes 12845056 | tf_op jit(solution)/shard_map/fp,bpn->bfn/dot_general | solution.py:96
  455.3 12.0 %add_bitcast_fusion = f32[64,512,64]{1,2,0:T(8,128)} fusion(f32[64,64,512]{2,1,0:T(8,128)} %fusion.29, f32[64,64,512]{2,1,0:T(8,128)} %fusion.31, f32[64,64,512]{2,1,0:T(8,128)S(1)} %fusion.30, bf16[64,256,64]{2,1,0:T(8,128)(2,1)S(1)} %bitcast.73, bf16[512,512]{1,0:T(8,128)(2,1)S(1)} %subtract_convert_fusion), kind=kOutput, calls=%fused_computation.4 | convolution fusion | flops 1080033280 | bytes 38010880 | tf_op jit(solution)/shard_map/fp,bpn->bfn/dot_general | solution.py:99
  467.3 6.7 %fusion.14 = f32[64,256,64]{1,2,0:T(8,128)} fusion(f32[64,512,64]{1,2,0:T(8,128)} %add_bitcast_fusion), kind=kLoop, calls=%fused_computation.18 | loop fusion | flops 3145728 | bytes 12582912 | tf_op jit(solution)/shard_map/add | solution.py:105
  (46 shorter events, 45.8 us)
Async XLA Ops:
  66.3 7.1 %copy-start.4 = (f32[1024]{0:T(1024)S(1)}, f32[1024]{0:T(1024)}, u32[]{:S(2)}) copy-start(f32[1024]{0:T(1024)} %param.11) | copy-start | bytes 12292
  66.3 7.1 %copy-start.5 = (s32[512]{0:T(512)S(1)}, s32[512]{0:T(512)}, u32[]{:S(2)}) copy-start(s32[512]{0:T(512)} %param.8) | copy-start | bytes 6148
  66.3 7.4 %copy-start.3 = (f32[2048]{0:T(1024)S(1)}, f32[2048]{0:T(1024)}, u32[]{:S(2)}) copy-start(f32[2048]{0:T(1024)} %param.9) | copy-start | bytes 24580
  66.3 7.4 %copy-start.2 = (f32[2,2048]{1,0:T(2,128)S(1)}, f32[2,2048]{1,0:T(2,128)}, u32[]{:S(2)}) copy-start(f32[2,2048]{1,0:T(2,128)} %param.10) | copy-start | bytes 49156
  66.3 145.3 %all-to-all-start = ((bf16[4,2,512,24,64]{2,4,3,1,0:T(8,128)(2,1)}), bf16[4,2,512,24,64]{2,4,3,1,0:T(8,128)(2,1)}, u32[]{:S(2)}, u32[]{:S(2)}) async-start(bf16[4,2,512,24,64]{2,4,3,1,0:T(8,128)(2,1)} %pad_maximum_fusion), calls=%async_computation | async-start | bytes 25165824 | tf_op jit(solution)/shard_map/all_to_all | solution.py:68
  244.9 21.4 %slice-start = ((s8[6291456]{0:T(1024)(128)(4,1)}), s8[4194304]{0:T(1024)(128)(4,1)S(1)}, s32[]{:S(2)}) async-start(s8[6291456]{0:T(1024)(128)(4,1)} %bitcast.81), calls=%async_computation.3 | async-start | bytes 8388608
  247.7 18.6 %copy-start.1 = (bf16[192,8,4,512]{3,1,2,0:T(8,128)(2,1)}, bf16[192,8,4,512]{3,1,2,0:T(8,128)(2,1)S(1)}, u32[]{:S(2)}) copy-start(bf16[192,8,4,512]{3,1,2,0:T(8,128)(2,1)S(1)} %copy.110) | copy-start | bytes 18874372
  247.7 18.6 %slice-start.1 = ((s8[6291456]{0:T(1024)(128)(4,1)}), s8[2097152]{0:T(1024)(128)(4,1)S(1)}, s32[]{:S(2)}) async-start(s8[6291456]{0:T(1024)(128)(4,1)} %bitcast.81), calls=%async_computation.4 | async-start | bytes 4194304
  304.4 72.0 %all-to-all-start.1 = ((bf16[8,2,65536]{2,1,0:T(2,128)(2,1)}), bf16[8,2,65536]{2,1,0:T(2,128)(2,1)S(1)}, u32[]{:S(2)}, u32[]{:S(2)}) async-start(bf16[8,2,65536]{2,1,0:T(2,128)(2,1)} %reshape.92), calls=%async_computation.1 | async-start | bytes 4194304 | tf_op jit(solution)/shard_map/all_to_all | solution.py:92
  376.5 54.2 %all-to-all-start.2 = ((bf16[8,2,65536]{2,1,0:T(2,128)(2,1)}), bf16[8,2,65536]{2,1,0:T(2,128)(2,1)}, u32[]{:S(2)}, u32[]{:S(2)}) async-start(bf16[8,2,65536]{2,1,0:T(2,128)(2,1)} %reshape.94), calls=%async_computation.2 | async-start | bytes 4194304 | tf_op jit(solution)/shard_map/all_to_all | solution.py:93
  441.6 2.4 copy-start
